TPU v7x, 32 devices: a whole 2x2x4 slice. The times are simulated.
32 devices in a mesh: ctx: 8 (over z, x), tp: 4 (over y, core).
Axes of the slice: x: 2, y: 2, z: 4, core: 2. Of those that a mesh axis runs over, the one named last changes fastest.
Arguments:
- queries: bfloat16 [1024, 8192], P(('ctx', 'tp')), may hold values from -6 to 6
- keys: bfloat16 [1024, 1024], P(('ctx', 'tp')), may hold values from -6 to 6
- values: bfloat16 [1024, 1024], P(('ctx', 'tp')), may hold values from -6 to 6
- doc_starts: int32 [14], replicated, may hold values from 0 to 1024, as said below
Outputs:
- attended: bfloat16 [1024, 8192], P(('ctx', 'tp'))
Inputs may be any that keep to these rules, and one draw needn't show every extreme that they name: `doc_starts`: nondecreasing and starting with 0; consecutive entries differ by at most 384, and some pair of consecutive entries below 1024 differs by exactly 384; the last document ends at 1024, and entries equal to 1024 stand for empty documents.
All inputs are finite; a program needn't handle non-finite values.
Results may differ from a plain program's by a relative error of at most 0.004.
Values may be sent and summed in bfloat16 or wider, within the bound.
A program may use at most 64 MiB of HBM per device.

v0:
```python
import jax
import jax.numpy as jnp
from jax import lax
from jax.sharding import PartitionSpec as P

QUERY_HEAD_COUNT = 64
KEY_VALUE_HEADS = 8
HEAD_WIDTH = 128


def passed_along(block, axis, distance):
    devices = range(lax.axis_size(axis))
    route = [(i - distance, i) for i in devices if i - distance in devices]
    return lax.ppermute(block, axis, route)


def doc_begin(positions, doc_starts):
    found = jnp.where(doc_starts[None, :] <= positions[:, None], doc_starts[None, :], 0)
    return jnp.max(found, axis=1)


def body(queries, keys, values, doc_starts):
    query_matrix, key_matrix, value_matrix = (
        lax.all_to_all(queries, "tp", split_axis=1, concat_axis=0, tiled=True),
        lax.all_to_all(keys, "tp", split_axis=1, concat_axis=0, tiled=True),
        lax.all_to_all(values, "tp", split_axis=1, concat_axis=0, tiled=True),
    )
    rows_per_block = query_matrix.shape[0]
    kv_local = key_matrix.shape[1] // HEAD_WIDTH
    query_groups = QUERY_HEAD_COUNT // KEY_VALUE_HEADS
    scale = HEAD_WIDTH ** (-0.5)
    reach_blocks = min(8, lax.axis_size("ctx") // 2)
    ctx_index = lax.axis_index("ctx")
    query_pos = ctx_index * rows_per_block + jnp.arange(rows_per_block, dtype=jnp.int32)
    begins = doc_begin(query_pos, doc_starts)
    query_heads = query_matrix.reshape(rows_per_block, kv_local, query_groups, HEAD_WIDTH)
    initial = (
        jnp.full((kv_local, query_groups, rows_per_block), -1e30, jnp.float32),
        jnp.zeros((kv_local, query_groups, rows_per_block), jnp.float32),
        jnp.zeros((kv_local, query_groups, rows_per_block, HEAD_WIDTH), jnp.float32),
    )

    def attend(state, pair, key_start):
        running_max, running_sum, accum = state
        key_tile = pair[0].reshape(rows_per_block, kv_local, HEAD_WIDTH)
        value_tile = pair[1].reshape(rows_per_block, kv_local, HEAD_WIDTH)
        scores = (
            jnp.einsum("qkgd,pkd->kgqp", query_heads, key_tile, preferred_element_type=jnp.float32)
            * scale
        )
        key_pos = key_start + jnp.arange(rows_per_block, dtype=jnp.int32)
        visible = (key_pos[None, :] <= query_pos[:, None]) & (key_pos[None, :] >= begins[:, None])
        scores = jnp.where(visible, scores, -1e30)
        new_max = jnp.maximum(running_max, jnp.max(scores, axis=-1))
        probs = jnp.where(visible, jnp.exp(scores - new_max[..., None]), 0.0)
        factor = jnp.exp(running_max - new_max)
        new_sum = running_sum * factor + jnp.sum(probs, axis=-1)
        update = jnp.einsum(
            "kgqp,pkd->kgqd",
            probs.astype(jnp.bfloat16),
            value_tile,
            preferred_element_type=jnp.float32,
        )
        return (new_max, new_sum, accum * factor[..., None] + update)

    paired = jnp.stack((key_matrix, value_matrix))
    visible_span = paired
    for level in range(reach_blocks.bit_length() - 1):
        farther = passed_along(visible_span, "ctx", 1 << level)
        visible_span = jnp.concatenate([visible_span, farther], axis=1)

    def visit(step, current):
        piece = lax.dynamic_slice_in_dim(
            visible_span, (step * rows_per_block).astype(jnp.int32), rows_per_block, 1
        )
        return attend(current, piece, (ctx_index - step) * rows_per_block)

    state = lax.fori_loop(0, reach_blocks, visit, initial)
    result = state[2] / state[1][..., None]
    result = (
        jnp.transpose(result, (2, 0, 1, 3))
        .reshape(rows_per_block, kv_local * query_groups * HEAD_WIDTH)
        .astype(jnp.bfloat16)
    )
    return lax.all_to_all(result, "tp", split_axis=0, concat_axis=1, tiled=True)


def solution(mesh):
    in_specs = (P(("ctx", "tp"), None), P(("ctx", "tp"), None), P(("ctx", "tp"), None), P())
    out_specs = P(("ctx", "tp"), None)
    return jax.shard_map(body, mesh=mesh, in_specs=in_specs, out_specs=out_specs, check_vma=False)
```

profile of v0, /device:TPU:0, one launch (start us, length us, event | category | flops | bytes accessed | tf_op | source)
XLA Modules:
  0.0 54.6 jit_solution(13648975216854075915)
XLA Ops:
  0.0 1.5 %copy.74 = bf16[4,4,8,256]{3,2,0,1:T(8,128)(2,1)} copy(bf16[4,4,8,256]{3,2,1,0:T(8,128)(2,1)} %bitcast.70) | data formatting | bytes 131072 | tf_op jit(solution)/shard_map/all_to_all | solution.py:25
  1.5 4.3 %all-to-all-start = ((bf16[32,4,256]{2,0,1:T(8,128)(2,1)}), bf16[32,4,256]{2,0,1:T(8,128)(2,1)S(1)}, u32[]{:S(2)}, u32[]{:S(2)}) async-start(bf16[32,4,256]{2,0,1:T(8,128)(2,1)} %bitcast.46), calls=%async_computation | async-start | bytes 131072 | tf_op jit(solution)/shard_map/all_to_all | solution.py:25
  5.8 0.8 %copy.73 = bf16[4,4,8,256]{3,2,0,1:T(8,128)(2,1)S(1)} copy(bf16[4,4,8,256]{3,2,1,0:T(8,128)(2,1)} %bitcast.71) | data formatting | bytes 131072 | tf_op jit(solution)/shard_map/all_to_all | solution.py:26
  6.6 3.3 %all-to-all-done = bf16[32,4,256]{2,0,1:T(8,128)(2,1)S(1)} async-done(((bf16[32,4,256]{2,0,1:T(8,128)(2,1)}), bf16[32,4,256]{2,0,1:T(8,128)(2,1)S(1)}, u32[]{:S(2)}, u32[]{:S(2)}) %all-to-all-start) | async-done | bytes 65568 | tf_op jit(solution)/shard_map/all_to_all | solution.py:25
  9.9 6.5 %all_to_all.64 = bf16[32,4,256]{2,0,1:T(8,128)(2,1)S(1)} all-to-all(bf16[32,4,256]{2,0,1:T(8,128)(2,1)S(1)} %bitcast.69), channel_id=1, replica_groups=mesh['ctx'=8,'tp'=4] {'tp'}, dimensions={1} | all-to-all | bytes 131072 | tf_op jit(solution)/shard_map/all_to_all | solution.py:26
  16.4 3.9 %collective-permute-start = (bf16[2,128,256]{2,1,0:T(8,128)(2,1)S(1)}, bf16[2,128,256]{2,1,0:T(8,128)(2,1)S(1)}, u32[]{:S(2)}, u32[]{:S(2)}) collective-permute-start(bf16[2,128,256]{2,1,0:T(8,128)(2,1)S(1)} %pad_maximum_fusion.2), channel_id=1, source_target_pairs={{0,4},{4,8},{8,12},{12,16},{16,20},{20,24},{24,28},{1,5},{5,9},{9,... | collective-permute-start | bytes 393224 | tf_op jit(solution)/shard_map/ppermute | solution.py:14
  20.3 0.0 copy-done
  20.3 0.8 %copy.72 = bf16[4,4,8,2048]{3,2,0,1:T(8,128)(2,1)} copy(bf16[4,4,8,2048]{3,2,1,0:T(8,128)(2,1)S(1)} %bitcast.68) | data formatting | bytes 1048576 | tf_op jit(solution)/shard_map/all_to_all | solution.py:24
  21.1 3.5 %all-to-all-start.2 = ((bf16[32,4,2048]{2,0,1:T(8,128)(2,1)}), bf16[32,4,2048]{2,0,1:T(8,128)(2,1)S(1)}, u32[]{:S(2)}, u32[]{:S(2)}) async-start(bf16[32,4,2048]{2,0,1:T(8,128)(2,1)} %bitcast.44), calls=%async_computation.2 | async-start | bytes 1048576 | tf_op jit(solution)/shard_map/all_to_all | solution.py:24
  24.6 0.0 collective-permute-done
  24.6 3.6 %collective-permute-start.1 = (bf16[2,256,256]{2,1,0:T(8,128)(2,1)S(1)}, bf16[2,256,256]{2,1,0:T(8,128)(2,1)S(1)}, u32[]{:S(2)}, u32[]{:S(2)}) collective-permute-start(bf16[2,256,256]{2,1,0:T(8,128)(2,1)S(1)} %pad_maximum_fusion.1), channel_id=1, source_target_pairs={{0,8},{4,12},{8,16},{12,20},{16,24},{20,28},{1,9},{5,13},{9,17},{1... | collective-permute-start | bytes 786440 | tf_op jit(solution)/shard_map/ppermute | solution.py:14
  28.3 0.0 copy-start.1
  28.3 0.6 %copy-done.1 = s32[14]{0:T(128)S(1)} copy-done((s32[14]{0:T(128)S(1)}, s32[14]{0:T(128)}, u32[]{:S(2)}) %copy-start.1) | copy-done | bytes 80
  28.9 0.1 select_reduce_fusion
  29.0 4.4 %all-to-all-done.2 = bf16[32,4,2048]{2,0,1:T(8,128)(2,1)S(1)} async-done(((bf16[32,4,2048]{2,0,1:T(8,128)(2,1)}), bf16[32,4,2048]{2,0,1:T(8,128)(2,1)S(1)}, u32[]{:S(2)}, u32[]{:S(2)}) %all-to-all-start.2) | async-done | bytes 524320 | tf_op jit(solution)/shard_map/all_to_all | solution.py:24
  33.4 0.1 copy.68
  33.5 0.1 copy.51
  33.7 0.6 %collective-permute-done.1 = bf16[2,256,256]{2,1,0:T(8,128)(2,1)S(1)} collective-permute-done((bf16[2,256,256]{2,1,0:T(8,128)(2,1)S(1)}, bf16[2,256,256]{2,1,0:T(8,128)(2,1)S(1)}, u32[]{:S(2)}, u32[]{:S(2)}) %collective-permute-start.1) | collective-permute-done | bytes 262176 | tf_op jit(solution)/shard_map/ppermute | solution.py:14
  34.3 7.0 %while.18 = (s32[]{:T(128)}, f32[2,8,128]{2,1,0:T(8,128)S(1)}, f32[2,8,128]{2,1,0:T(8,128)S(1)}, f32[2,8,128,128]{3,2,1,0:T(8,128)S(1)}, s32[]{:T(128)}, /*index...) while((s32[]{:T(128)}, f32[2,8,128]{2,1,0:T(8,128)S(1)}, ...), condition=%wide.region_4.5_spmd.clone, body=%wide.region_1.4_spmd.clone.sunk | while | flops 137423104 | bytes 6621947 | solution.py:78
  34.4 0.1 compare_and_fusion.2
  34.5 0.1 copy.77
  34.6 0.1 copy.78
  34.7 0.4 fusion.28
  35.1 0.2 fusion.29
  35.3 0.7 %convolution_add_fusion.2 = f32[2,8,128,128]{3,2,1,0:T(8,128)S(1)} fusion(bf16[128,2,128,1]{0,2,3,1:T(8,128)(2,1)S(1)} %bitcast.57, f32[2,8,128,128]{3,2,1,0:T(8,128)S(1)} %get-tuple-element.354, f32[2,8,128,128]{2,3,1,0:T(8,128)S(1)} %get-tuple-element.333, f32[2,8,128]{2,1,0:T(8,128)S(1)} %get-tuple-element.336, ...), kind=kOutput, calls=%fused_computation.1.clone.1 | convolution fusion | flops 68681728 | bytes 3244033 | tf_op jit(solution)/shard_map/while/body/eval_jaxpr/kgqp,pkd->kgqd/dot_general | solution.py:58
  36.1 0.1 compare_and_fusion.2
  36.2 0.1 copy.77
  36.4 0.1 copy.78
  36.5 0.4 fusion.28
  36.9 0.2 fusion.29
  37.1 0.7 %convolution_add_fusion.2 = f32[2,8,128,128]{3,2,1,0:T(8,128)S(1)} fusion(bf16[128,2,128,1]{0,2,3,1:T(8,128)(2,1)S(1)} %bitcast.57, f32[2,8,128,128]{3,2,1,0:T(8,128)S(1)} %get-tuple-element.354, f32[2,8,128,128]{2,3,1,0:T(8,128)S(1)} %get-tuple-element.333, f32[2,8,128]{2,1,0:T(8,128)S(1)} %get-tuple-element.336, ...), kind=kOutput, calls=%fused_computation.1.clone.1 | convolution fusion | flops 68681728 | bytes 3244033 | tf_op jit(solution)/shard_map/while/body/eval_jaxpr/kgqp,pkd->kgqd/dot_general | solution.py:58
  37.9 0.1 compare_and_fusion.2
  38.0 0.1 copy.77
  38.1 0.1 copy.78
  38.2 0.4 fusion.28
  38.6 0.2 fusion.29
  38.8 0.7 %convolution_add_fusion.2 = f32[2,8,128,128]{3,2,1,0:T(8,128)S(1)} fusion(bf16[128,2,128,1]{0,2,3,1:T(8,128)(2,1)S(1)} %bitcast.57, f32[2,8,128,128]{3,2,1,0:T(8,128)S(1)} %get-tuple-element.354, f32[2,8,128,128]{2,3,1,0:T(8,128)S(1)} %get-tuple-element.333, f32[2,8,128]{2,1,0:T(8,128)S(1)} %get-tuple-element.336, ...), kind=kOutput, calls=%fused_computation.1.clone.1 | convolution fusion | flops 68681728 | bytes 3244033 | tf_op jit(solution)/shard_map/while/body/eval_jaxpr/kgqp,pkd->kgqd/dot_general | solution.py:58
  39.6 0.1 compare_and_fusion.2
  39.7 0.1 copy.77
  39.8 0.1 copy.78
  40.0 0.4 fusion.28
  40.3 0.2 fusion.29
  40.6 0.7 %convolution_add_fusion.2 = f32[2,8,128,128]{3,2,1,0:T(8,128)S(1)} fusion(bf16[128,2,128,1]{0,2,3,1:T(8,128)(2,1)S(1)} %bitcast.57, f32[2,8,128,128]{3,2,1,0:T(8,128)S(1)} %get-tuple-element.354, f32[2,8,128,128]{2,3,1,0:T(8,128)S(1)} %get-tuple-element.333, f32[2,8,128]{2,1,0:T(8,128)S(1)} %get-tuple-element.336, ...), kind=kOutput, calls=%fused_computation.1.clone.1 | convolution fusion | flops 68681728 | bytes 3244033 | tf_op jit(solution)/shard_map/while/body/eval_jaxpr/kgqp,pkd->kgqd/dot_general | solution.py:58
  41.3 0.3 fusion.12
  41.7 0.3 copy.52
  42.0 0.2 convert_element_type.19
  42.2 11.5 %all_to_all.65 = bf16[4,32,2048]{2,1,0:T(8,128)(2,1)S(1)} all-to-all(bf16[4,32,2048]{2,1,0:T(8,128)(2,1)S(1)} %convert_element_type.19), channel_id=1, replica_groups=mesh['ctx'=8,'tp'=4] {'tp'}, dimensions={0} | all-to-all | bytes 1048576 | tf_op jit(solution)/shard_map/all_to_all | solution.py:85
  53.8 0.8 %copy.67 = bf16[4,4,8,2048]{3,2,0,1:T(8,128)(2,1)} copy(bf16[4,4,8,2048]{3,2,1,0:T(8,128)(2,1)S(1)} %bitcast.61) | data formatting | bytes 1048576 | tf_op jit(solution)/shard_map/all_to_all | solution.py:85
  (28 shorter events, 0.3 us)
Async XLA Ops:
  0.0 20.3 %copy-start = (bf16[32,8192]{1,0:T(8,128)(2,1)S(1)}, bf16[32,8192]{1,0:T(8,128)(2,1)}, u32[]{:S(2)}) copy-start(bf16[32,8192]{1,0:T(8,128)(2,1)} %param.6) | copy-start | bytes 1572868
  1.5 8.4 %all-to-all-start = ((bf16[32,4,256]{2,0,1:T(8,128)(2,1)}), bf16[32,4,256]{2,0,1:T(8,128)(2,1)S(1)}, u32[]{:S(2)}, u32[]{:S(2)}) async-start(bf16[32,4,256]{2,0,1:T(8,128)(2,1)} %bitcast.46), calls=%async_computation | async-start | bytes 131072 | tf_op jit(solution)/shard_map/all_to_all | solution.py:25
  16.4 8.2 %collective-permute-start = (bf16[2,128,256]{2,1,0:T(8,128)(2,1)S(1)}, bf16[2,128,256]{2,1,0:T(8,128)(2,1)S(1)}, u32[]{:S(2)}, u32[]{:S(2)}) collective-permute-start(bf16[2,128,256]{2,1,0:T(8,128)(2,1)S(1)} %pad_maximum_fusion.2), channel_id=1, source_target_pairs={{0,4},{4,8},{8,12},{12,16},{16,20},{20,24},{24,28},{1,5},{5,9},{9,... | collective-permute-start | bytes 393224 | tf_op jit(solution)/shard_map/ppermute | solution.py:14
  21.1 12.3 %all-to-all-start.2 = ((bf16[32,4,2048]{2,0,1:T(8,128)(2,1)}), bf16[32,4,2048]{2,0,1:T(8,128)(2,1)S(1)}, u32[]{:S(2)}, u32[]{:S(2)}) async-start(bf16[32,4,2048]{2,0,1:T(8,128)(2,1)} %bitcast.44), calls=%async_computation.2 | async-start | bytes 1048576 | tf_op jit(solution)/shard_map/all_to_all | solution.py:24
  24.6 9.7 %collective-permute-start.1 = (bf16[2,256,256]{2,1,0:T(8,128)(2,1)S(1)}, bf16[2,256,256]{2,1,0:T(8,128)(2,1)S(1)}, u32[]{:S(2)}, u32[]{:S(2)}) collective-permute-start(bf16[2,256,256]{2,1,0:T(8,128)(2,1)S(1)} %pad_maximum_fusion.1), channel_id=1, source_target_pairs={{0,8},{4,12},{8,16},{12,20},{16,24},{20,28},{1,9},{5,13},{9,17},{1... | collective-permute-start | bytes 786440 | tf_op jit(solution)/shard_map/ppermute | solution.py:14
  28.3 0.7 %copy-start.1 = (s32[14]{0:T(128)S(1)}, s32[14]{0:T(128)}, u32[]{:S(2)}) copy-start(s32[14]{0:T(128)} %param.9) | copy-start | bytes 172
where the time goes:
time: 55 us; the launch traced here: 54.6 us
  blocking collectives  18 us (33%)
  starting transfers between devices  15.2 us (28%)
  waiting for transfers between devices  8.29 us (15%)
  local copies, waits for them, and re-layouts  6.49 us (12%)
  matrix products  4.32 us (8%)
  other arithmetic  1.73 us (3%)
    all_to_all x1, blocking collectives, body(): return lax.all_to_all(result, 'tp', split_axis=0, concat_axis=1, tiled=True)  11.5 us
    ppermute x2, starting transfers between devices, passed_along(): return lax.ppermute(block, axis, route)  7.46 us
    all_to_all x1, blocking collectives, body(): lax.all_to_all(values, 'tp', split_axis=1, concat_axis=0, tiled=True)  6.47 us
    all_to_all x1, waiting for transfers between devices, body(): lax.all_to_all(queries, 'tp', split_axis=1, concat_axis=0, tiled=True)  4.36 us
    all_to_all x1, starting transfers between devices, body(): lax.all_to_all(keys, 'tp', split_axis=1, concat_axis=0, tiled=True)  4.26 us
    all_to_all x1, starting transfers between devices, body(): lax.all_to_all(queries, 'tp', split_axis=1, concat_axis=0, tiled=True)  3.47 us
    all_to_all x1, waiting for transfers between devices, body(): lax.all_to_all(keys, 'tp', split_axis=1, concat_axis=0, tiled=True)  3.28 us
    dot_general x4, matrix products, attend(): jnp.einsum('kgqp,pkd->kgqd', probs.astype(jnp.bfloat16), value_tile, pref...  2.85 us
  transfers between devices with their start and end apart: 4, of which 3 were waited for; matrix products, arithmetic and copies ran while one was open for 4% of the time, Pallas kernels for 0%

commit v1 on v0

v1 whole, which is shorter than its diff:
```python
import functools
import math

import jax
import jax.numpy as jnp
from jax import lax
from jax.experimental import pallas as pl
from jax.experimental.pallas import tpu as pltpu
from jax.sharding import PartitionSpec as P

QUERY_HEAD_COUNT = 64
KEY_VALUE_HEADS = 8
HEAD_WIDTH = 128
CORES = 2
MESH = pl.DeviceIdType.MESH


def plan(n_ctx, n_tp):
    span = n_tp // CORES
    across = span if n_ctx % span == 0 else 1
    in_plane = span * across
    planes = n_ctx * n_tp // CORES // in_plane
    reach_blocks = min(8, n_ctx // 2)
    reach = (reach_blocks - 1) * n_tp // CORES
    return in_plane, planes, reach


def kernel(n_ctx, n_tp, n_docs, docs, q_hbm, k_hbm, v_hbm, o_ref, q_buf, kv, bias, local_sem, send_sem, recv_sem):
    in_plane, planes, reach = plan(n_ctx, n_tp)
    levels = (reach + in_plane - 1) // in_plane
    rows = k_hbm.shape[0]
    width = k_hbm.shape[1]
    me = lax.axis_index("ctx") * n_tp + lax.axis_index("tp")
    core, chip = lax.rem(me, CORES), lax.div(me, CORES)
    plane, spot = lax.div(chip, in_plane), lax.rem(chip, in_plane)

    def device(other_chip, other_core):
        index = other_chip * CORES + other_core
        return (lax.div(index, n_tp), lax.rem(index, n_tp))

    def piece(distance, from_core):
        return CORES * (reach - distance) + from_core

    transit = CORES * (reach + 1)

    def part(index):
        return kv.at[pl.ds(pl.multiple_of(index * rows, rows), rows), :]

    own = piece(0, core)
    own_rows = pl.ds(pl.multiple_of(own * rows, rows), rows)
    load_k = pltpu.make_async_copy(k_hbm, kv.at[own_rows, pl.ds(0, width)], local_sem.at[0])
    load_v = pltpu.make_async_copy(v_hbm, kv.at[own_rows, pl.ds(width, width)], local_sem.at[1])
    load_q = pltpu.make_async_copy(q_hbm, q_buf, local_sem.at[2])
    load_k.start()
    load_v.start()
    load_q.start()

    partner = device(chip, 1 - core)
    around = [lax.rem(spot + o, in_plane) for o in range(1, in_plane)]
    barrier = pltpu.get_barrier_semaphore()
    pl.semaphore_signal(barrier, inc=1, device_id=partner, device_id_type=MESH)
    for other in around:
        pl.semaphore_signal(
            barrier, inc=1, device_id=device(plane * in_plane + other, core), device_id_type=MESH
        )
    below, above = plane > 0, plane < planes - 1

    @pl.when(below)
    def _():
        pl.semaphore_signal(
            barrier, inc=1, device_id=device(chip - in_plane, core), device_id_type=MESH
        )

    @pl.when(above)
    def _():
        pl.semaphore_signal(
            barrier, inc=1, device_id=device(chip + in_plane, core), device_id_type=MESH
        )

    sent = []

    def send(when, source, target, target_index):
        copy = pltpu.make_async_remote_copy(
            src_ref=part(source),
            dst_ref=part(target_index),
            send_sem=send_sem.at[len(sent)],
            recv_sem=recv_sem.at[target_index],
            device_id=target,
            device_id_type=MESH,
        )
        sent.append((when, copy))
        pl.when(when)(copy.start)

    def arrived(when, index):
        copy = pltpu.make_async_copy(part(index), part(index), recv_sem.at[index])
        pl.when(when)(copy.wait)

    for distance in range(1, reach + 1):
        @pl.when(chip < distance)
        def _():
            first = piece(distance, 0) * rows
            kv[pl.ds(first, CORES * rows), :] = jnp.zeros((CORES * rows, 2 * width), kv.dtype)

    pl.semaphore_wait(
        barrier, in_plane + below.astype(jnp.int32) + above.astype(jnp.int32)
    )
    load_k.wait()
    load_v.wait()

    def forwards(level, source, held):
        distance = level * in_plane
        if level < levels:
            following = distance + in_plane
            index = piece(following, core) if following <= reach else transit + core
            needed = following - spot <= reach
            send(held & above & needed, source, device(chip + in_plane, core), index)
        for other in around:
            away = distance + other - spot
            send(
                held & (away >= 1) & (away <= reach),
                source,
                device(plane * in_plane + other, core),
                piece(jnp.clip(away, 1, reach), core),
            )
        if distance <= reach:
            send(held, source, partner, piece(distance, core))

    def pass_to_partner(when, distance):
        index = piece(distance, core)
        arrived(when, index)
        send(when, index, partner, index)

    forwards(0, own, chip >= 0)

    keys = CORES * rows * (reach + 1)
    query_pos = me * rows + lax.broadcasted_iota(jnp.int32, (rows, keys), 0)
    key_pos = (chip - reach) * (CORES * rows) + lax.broadcasted_iota(jnp.int32, (rows, keys), 1)
    token = me * rows + lax.broadcasted_iota(jnp.int32, (rows, 1), 0)
    begin = jnp.zeros((rows, 1), jnp.int32)
    for doc in range(n_docs):
        start = docs[doc]
        begin = jnp.maximum(begin, jnp.where(start <= token, start, 0))
    visible = (key_pos <= query_pos) & (key_pos >= begin)
    bias[...] = jnp.where(visible, 0.0, -1e30)
    load_q.wait()

    for level in range(1, levels + 1):
        distance = level * in_plane
        index = piece(distance, core) if distance <= reach else transit + core
        held = (plane >= level) & (distance - spot <= reach)
        if level > 1:
            for back in range(1, min(reach, (level - 1) * in_plane - 1) + 1):
                if back % in_plane:
                    origin = lax.div(spot - back + 4 * in_plane, in_plane) - 4
                    pass_to_partner((chip >= back) & (origin == 2 - level), back)
        arrived(held, index)
        forwards(level, index, held)
    for back in range(1, reach + 1):
        if back % in_plane:
            origin = lax.div(spot - back + 4 * in_plane, in_plane) - 4
            pass_to_partner((chip >= back) & (origin <= 1 - levels), back)
    for distance in range(reach + 1):
        arrived(chip >= distance, piece(distance, 1 - core))

    group = QUERY_HEAD_COUNT // KEY_VALUE_HEADS
    factor = HEAD_WIDTH ** (-0.5) * math.log2(math.e)

    def head(g, carry):
        first = pl.multiple_of(g * (group * HEAD_WIDTH), group * HEAD_WIDTH)
        queries = jnp.concatenate(
            [q_buf[:, pl.ds(first + h * HEAD_WIDTH, HEAD_WIDTH)] for h in range(group)], axis=0
        )
        at = pl.multiple_of(g * HEAD_WIDTH, HEAD_WIDTH)
        key = kv[pl.ds(0, keys), pl.ds(at, HEAD_WIDTH)]
        value = kv[pl.ds(0, keys), pl.ds(width + at, HEAD_WIDTH)]
        scores = lax.dot_general(
            queries, key, (((1,), (1,)), ((), ())), preferred_element_type=jnp.float32
        )
        scores = (scores.reshape(group, rows, keys) + bias[...][None]).reshape(group * rows, keys)
        top = jnp.max(scores, axis=1, keepdims=True)
        probs = jnp.exp2((scores - top) * factor)
        total = jnp.sum(probs, axis=1, keepdims=True)
        out = jnp.dot(probs.astype(jnp.bfloat16), value, preferred_element_type=jnp.float32)
        out = (out / total).astype(jnp.bfloat16)
        for h in range(group):
            o_ref[:, pl.ds(first + h * HEAD_WIDTH, HEAD_WIDTH)] = out[h * rows : (h + 1) * rows]
        return carry

    lax.fori_loop(0, KEY_VALUE_HEADS, head, 0)
    for when, copy in sent:
        pl.when(when)(copy.wait_send)


def body(n_ctx, n_tp, queries, keys, values, doc_starts):
    in_plane, planes, reach = plan(n_ctx, n_tp)
    levels = (reach + in_plane - 1) // in_plane
    rows, width = keys.shape
    pieces = CORES * (reach + 2)
    copies = (levels + 1) * (in_plane + 1) + levels * (reach + 1)
    return pl.pallas_call(
        functools.partial(kernel, n_ctx, n_tp, doc_starts.shape[0]),
        out_shape=jax.ShapeDtypeStruct(queries.shape, queries.dtype),
        in_specs=[pl.BlockSpec(memory_space=pltpu.SMEM)]
        + [pl.BlockSpec(memory_space=pl.ANY)] * 3,
        out_specs=pl.BlockSpec(memory_space=pltpu.VMEM),
        scratch_shapes=[
            pltpu.VMEM(queries.shape, queries.dtype),
            pltpu.VMEM((pieces * rows, 2 * width), keys.dtype),
            pltpu.VMEM((rows, CORES * rows * (reach + 1)), jnp.float32),
            pltpu.SemaphoreType.DMA((3,)),
            pltpu.SemaphoreType.DMA((copies,)),
            pltpu.SemaphoreType.DMA((pieces,)),
        ],
        compiler_params=pltpu.CompilerParams(collective_id=0, has_side_effects=True),
    )(doc_starts, queries, keys, values)


def solution(mesh):
    n_ctx, n_tp = mesh.shape["ctx"], mesh.shape["tp"]
    in_specs = (P(("ctx", "tp"), None), P(("ctx", "tp"), None), P(("ctx", "tp"), None), P())
    return jax.shard_map(
        functools.partial(body, n_ctx, n_tp),
        mesh=mesh,
        in_specs=in_specs,
        out_specs=P(("ctx", "tp"), None),
        check_vma=False,
    )
```

time: 55 us -> 27.3 us (0.50)
  the two profiles are of different devices: /device:TPU:0 before, /device:TPU:17 now
where the time goes in v1:
time: 27.3 us; the launch traced here: 26.9 us
  Pallas kernels  25 us (92%)
  local copies, waits for them, and re-layouts  1.87 us (7%)
    pallas_call x1, Pallas kernels, body(): pl.pallas_call(functools.partial(kernel, n_ctx, n_tp, doc_starts.shape[0]...  25 us
    unnamed x1, local copies, waits for them, and re-layouts  1.87 us

profile of v1, /device:TPU:17, one launch (start us, length us, event | category | flops | bytes accessed | tf_op | source)
XLA Modules:
  0.0 26.9 jit_solution(1788561855301557788)
XLA Ops:
  0.0 25.0 %shard_map.46 = bf16[32,8192]{1,0:T(8,128)(2,1)} custom-call(s32[14]{0:T(128)} %docs.1, bf16[32,8192]{1,0:T(8,128)(2,1)} %q_hbm.1, bf16[32,1024]{1,0:T(8,128)(2,1)} %k_hbm.1, bf16[32,1024]{1,0:T(8,128)(2,1)} %v_hbm.1), custom_call_target="tpu_custom_call" | custom-call | tf_op jit(solution)/shard_map/pallas_call | solution.py:200
  25.0 1.9 %copy.6 = bf16[32,8192]{1,0:T(8,128)(2,1)} copy(bf16[32,8192]{1,0:T(8,128)(2,1)} %shard_map.46) | data formatting | bytes 1048576

commit v2 on v1

--- a/solution.py
+++ b/solution.py
@@ -12,6 +12,8 @@
 KEY_VALUE_HEADS = 8
 HEAD_WIDTH = 128
 CORES = 2
+ROW_CUTS = 2
+CHUNKS = 2 * ROW_CUTS
 MESH = pl.DeviceIdType.MESH
 
 
@@ -43,8 +45,14 @@
 
     transit = CORES * (reach + 1)
 
-    def part(index):
-        return kv.at[pl.ds(pl.multiple_of(index * rows, rows), rows), :]
+    tall = rows // ROW_CUTS
+
+    def part(index, chunk):
+        cut, side = chunk % ROW_CUTS, chunk // ROW_CUTS
+        return kv.at[
+            pl.ds(pl.multiple_of(index * rows + cut * tall, tall), tall),
+            pl.ds(side * width, width),
+        ]
 
     own = piece(0, core)
     own_rows = pl.ds(pl.multiple_of(own * rows, rows), rows)
@@ -79,20 +87,21 @@
 
     sent = []
 
-    def send(when, source, target, target_index):
+    def send(when, chunk, source, target, target_index):
         copy = pltpu.make_async_remote_copy(
-            src_ref=part(source),
-            dst_ref=part(target_index),
+            src_ref=part(source, chunk),
+            dst_ref=part(target_index, chunk),
             send_sem=send_sem.at[len(sent)],
-            recv_sem=recv_sem.at[target_index],
+            recv_sem=recv_sem.at[target_index, chunk],
             device_id=target,
             device_id_type=MESH,
         )
         sent.append((when, copy))
         pl.when(when)(copy.start)
 
-    def arrived(when, index):
-        copy = pltpu.make_async_copy(part(index), part(index), recv_sem.at[index])
+    def arrived(when, index, chunk):
+        place = part(index, chunk)
+        copy = pltpu.make_async_copy(place, place, recv_sem.at[index, chunk])
         pl.when(when)(copy.wait)
 
     for distance in range(1, reach + 1):
@@ -104,33 +113,37 @@
     pl.semaphore_wait(
         barrier, in_plane + below.astype(jnp.int32) + above.astype(jnp.int32)
     )
-    load_k.wait()
-    load_v.wait()
-
-    def forwards(level, source, held):
+
+    def forwards(level, source, held, chunk):
         distance = level * in_plane
         if level < levels:
             following = distance + in_plane
             index = piece(following, core) if following <= reach else transit + core
             needed = following - spot <= reach
-            send(held & above & needed, source, device(chip + in_plane, core), index)
+            send(held & above & needed, chunk, source, device(chip + in_plane, core), index)
         for other in around:
             away = distance + other - spot
             send(
                 held & (away >= 1) & (away <= reach),
+                chunk,
                 source,
                 device(plane * in_plane + other, core),
                 piece(jnp.clip(away, 1, reach), core),
             )
         if distance <= reach:
-            send(held, source, partner, piece(distance, core))
+            send(held, chunk, source, partner, piece(distance, core))
 
     def pass_to_partner(when, distance):
         index = piece(distance, core)
-        arrived(when, index)
-        send(when, index, partner, index)
-
-    forwards(0, own, chip >= 0)
+        for chunk in range(CHUNKS):
+            arrived(when, index, chunk)
+            send(when, chunk, index, partner, index)
+
+    load_k.wait()
+    for chunk in range(CHUNKS):
+        if chunk == ROW_CUTS:
+            load_v.wait()
+        forwards(0, own, chip >= 0, chunk)
 
     keys = CORES * rows * (reach + 1)
     query_pos = me * rows + lax.broadcasted_iota(jnp.int32, (rows, keys), 0)
@@ -153,40 +166,41 @@
                 if back % in_plane:
                     origin = lax.div(spot - back + 4 * in_plane, in_plane) - 4
                     pass_to_partner((chip >= back) & (origin == 2 - level), back)
-        arrived(held, index)
-        forwards(level, index, held)
+        for chunk in range(CHUNKS):
+            arrived(held, index, chunk)
+            forwards(level, index, held, chunk)
     for back in range(1, reach + 1):
         if back % in_plane:
             origin = lax.div(spot - back + 4 * in_plane, in_plane) - 4
             pass_to_partner((chip >= back) & (origin <= 1 - levels), back)
     for distance in range(reach + 1):
-        arrived(chip >= distance, piece(distance, 1 - core))
+        for chunk in range(CHUNKS):
+            arrived(chip >= distance, piece(distance, 1 - core), chunk)
 
     group = QUERY_HEAD_COUNT // KEY_VALUE_HEADS
     factor = HEAD_WIDTH ** (-0.5) * math.log2(math.e)
 
-    def head(g, carry):
-        first = pl.multiple_of(g * (group * HEAD_WIDTH), group * HEAD_WIDTH)
+    ones = jnp.ones((keys, HEAD_WIDTH), jnp.bfloat16)
+    hidden = bias[...][None]
+    for g in range(KEY_VALUE_HEADS):
+        first = g * group * HEAD_WIDTH
         queries = jnp.concatenate(
             [q_buf[:, pl.ds(first + h * HEAD_WIDTH, HEAD_WIDTH)] for h in range(group)], axis=0
         )
-        at = pl.multiple_of(g * HEAD_WIDTH, HEAD_WIDTH)
-        key = kv[pl.ds(0, keys), pl.ds(at, HEAD_WIDTH)]
-        value = kv[pl.ds(0, keys), pl.ds(width + at, HEAD_WIDTH)]
+        key = kv[pl.ds(0, keys), pl.ds(g * HEAD_WIDTH, HEAD_WIDTH)]
+        value = kv[pl.ds(0, keys), pl.ds(width + g * HEAD_WIDTH, HEAD_WIDTH)]
         scores = lax.dot_general(
             queries, key, (((1,), (1,)), ((), ())), preferred_element_type=jnp.float32
         )
-        scores = (scores.reshape(group, rows, keys) + bias[...][None]).reshape(group * rows, keys)
+        scores = (scores.reshape(group, rows, keys) + hidden).reshape(group * rows, keys)
         top = jnp.max(scores, axis=1, keepdims=True)
-        probs = jnp.exp2((scores - top) * factor)
-        total = jnp.sum(probs, axis=1, keepdims=True)
-        out = jnp.dot(probs.astype(jnp.bfloat16), value, preferred_element_type=jnp.float32)
-        out = (out / total).astype(jnp.bfloat16)
+        probs = jnp.exp2((scores - top) * factor).astype(jnp.bfloat16)
+        both = jnp.dot(
+            probs, jnp.concatenate([value, ones], axis=1), preferred_element_type=jnp.float32
+        )
+        out = (both[:, :HEAD_WIDTH] / both[:, HEAD_WIDTH:]).astype(jnp.bfloat16)
         for h in range(group):
             o_ref[:, pl.ds(first + h * HEAD_WIDTH, HEAD_WIDTH)] = out[h * rows : (h + 1) * rows]
-        return carry
-
-    lax.fori_loop(0, KEY_VALUE_HEADS, head, 0)
     for when, copy in sent:
         pl.when(when)(copy.wait_send)
 
@@ -201,17 +215,17 @@
         functools.partial(kernel, n_ctx, n_tp, doc_starts.shape[0]),
         out_shape=jax.ShapeDtypeStruct(queries.shape, queries.dtype),
         in_specs=[pl.BlockSpec(memory_space=pltpu.SMEM)]
-        + [pl.BlockSpec(memory_space=pl.ANY)] * 3,
+        + [pl.BlockSpec(memory_space=pltpu.HBM)] * 3,
         out_specs=pl.BlockSpec(memory_space=pltpu.VMEM),
         scratch_shapes=[
             pltpu.VMEM(queries.shape, queries.dtype),
             pltpu.VMEM((pieces * rows, 2 * width), keys.dtype),
             pltpu.VMEM((rows, CORES * rows * (reach + 1)), jnp.float32),
             pltpu.SemaphoreType.DMA((3,)),
-            pltpu.SemaphoreType.DMA((copies,)),
-            pltpu.SemaphoreType.DMA((pieces,)),
+            pltpu.SemaphoreType.DMA((copies * CHUNKS,)),
+            pltpu.SemaphoreType.DMA((pieces, CHUNKS)),
         ],
-        compiler_params=pltpu.CompilerParams(collective_id=0, has_side_effects=True),
+        compiler_params=pltpu.CompilerParams(collective_id=0, has_side_effects=True, vmem_limit_bytes=16 << 20),
     )(doc_starts, queries, keys, values)
 
 

time: 27.3 us -> 26.8 us (0.982)
  Pallas kernels: 25 us -> 22.4 us
  local copies, waits for them, and re-layouts: 1.87 us -> 4.17 us
    pallas_call x1, Pallas kernels: 25 us -> 22.4 us  [body(): pl.pallas_call(functools.partial(kernel, n_ctx, n_tp, doc_starts.shape[0]...]
    unnamed x1 -> x9, local copies, waits for them, and re-layouts: 1.87 us -> 4.17 us
where the time goes in v2:
time: 26.8 us; the launch traced here: 26.6 us
  Pallas kernels  22.4 us (84%)
  local copies, waits for them, and re-layouts  4.17 us (16%)
    pallas_call x1, Pallas kernels, body(): pl.pallas_call(functools.partial(kernel, n_ctx, n_tp, doc_starts.shape[0]...  22.4 us
    unnamed x9, local copies, waits for them, and re-layouts  4.17 us

profile of v2, /device:TPU:17, one launch (start us, length us, event | category | flops | bytes accessed | tf_op | source)
XLA Modules:
  0.0 26.6 jit_solution(6756109069371012908)
XLA Ops:
  0.0 0.0 copy-start
  0.0 1.0 %copy-done = bf16[32,8192]{1,0:T(8,128)(2,1)S(1)} copy-done((bf16[32,8192]{1,0:T(8,128)(2,1)S(1)}, bf16[32,8192]{1,0:T(8,128)(2,1)}, u32[]{:S(2)}) %copy-start) | copy-done | bytes 524312
  1.0 0.0 copy-start.1
  1.0 0.8 %copy-done.1 = bf16[32,1024]{1,0:T(8,128)(2,1)S(1)} copy-done((bf16[32,1024]{1,0:T(8,128)(2,1)S(1)}, bf16[32,1024]{1,0:T(8,128)(2,1)}, u32[]{:S(2)}) %copy-start.1) | copy-done | bytes 65560
  1.9 0.0 copy-start.2
  1.9 0.8 %copy-done.2 = bf16[32,1024]{1,0:T(8,128)(2,1)S(1)} copy-done((bf16[32,1024]{1,0:T(8,128)(2,1)S(1)}, bf16[32,1024]{1,0:T(8,128)(2,1)}, u32[]{:S(2)}) %copy-start.2) | copy-done | bytes 65560
  2.7 0.0 copy-start.3
  2.7 0.7 %copy-done.3 = s32[14]{0:T(128)S(1)} copy-done((s32[14]{0:T(128)S(1)}, s32[14]{0:T(128)}, u32[]{:S(2)}) %copy-start.3) | copy-done | bytes 80
  3.4 22.4 %shard_map.46 = bf16[32,8192]{1,0:T(8,128)(2,1)S(1)} custom-call(s32[14]{0:T(128)S(1)} %copy-done.3, bf16[32,8192]{1,0:T(8,128)(2,1)S(1)} %copy-done, bf16[32,1024]{1,0:T(8,128)(2,1)S(1)} %copy-done.1, bf16[32,1024]{1,0:T(8,128)(2,1)S(1)} %copy-done.2), custom_call_target="tpu_custom_call" | custom-call | tf_op jit(solution)/shard_map/pallas_call | solution.py:214
  25.8 0.8 %copy.6 = bf16[32,8192]{1,0:T(8,128)(2,1)} copy(bf16[32,8192]{1,0:T(8,128)(2,1)S(1)} %shard_map.46) | data formatting | bytes 1048576
Async XLA Ops:
  0.0 1.0 %copy-start = (bf16[32,8192]{1,0:T(8,128)(2,1)S(1)}, bf16[32,8192]{1,0:T(8,128)(2,1)}, u32[]{:S(2)}) copy-start(bf16[32,8192]{1,0:T(8,128)(2,1)} %q_hbm.1) | copy-start | bytes 1572868
  1.0 0.8 %copy-start.1 = (bf16[32,1024]{1,0:T(8,128)(2,1)S(1)}, bf16[32,1024]{1,0:T(8,128)(2,1)}, u32[]{:S(2)}) copy-start(bf16[32,1024]{1,0:T(8,128)(2,1)} %k_hbm.1) | copy-start | bytes 196612
  1.9 0.8 %copy-start.2 = (bf16[32,1024]{1,0:T(8,128)(2,1)S(1)}, bf16[32,1024]{1,0:T(8,128)(2,1)}, u32[]{:S(2)}) copy-start(bf16[32,1024]{1,0:T(8,128)(2,1)} %v_hbm.1) | copy-start | bytes 196612
  2.7 0.7 %copy-start.3 = (s32[14]{0:T(128)S(1)}, s32[14]{0:T(128)}, u32[]{:S(2)}) copy-start(s32[14]{0:T(128)} %docs.1) | copy-start | bytes 172

commit v3 on v2

--- a/solution.py
+++ b/solution.py
@@ -14,27 +14,25 @@
 CORES = 2
 ROW_CUTS = 2
 CHUNKS = 2 * ROW_CUTS
+VMEM_BYTES = 67043328 - 540 * 1024
 MESH = pl.DeviceIdType.MESH
 
 
 def plan(n_ctx, n_tp):
-    span = n_tp // CORES
-    across = span if n_ctx % span == 0 else 1
-    in_plane = span * across
-    planes = n_ctx * n_tp // CORES // in_plane
-    reach_blocks = min(8, n_ctx // 2)
-    reach = (reach_blocks - 1) * n_tp // CORES
-    return in_plane, planes, reach
+    deep = n_tp // CORES
+    across = deep if n_ctx % deep == 0 else 1
+    return deep, across, n_ctx // across, min(8, n_ctx // 2) - 1
 
 
 def kernel(n_ctx, n_tp, n_docs, docs, q_hbm, k_hbm, v_hbm, o_ref, q_buf, kv, bias, local_sem, send_sem, recv_sem):
-    in_plane, planes, reach = plan(n_ctx, n_tp)
-    levels = (reach + in_plane - 1) // in_plane
+    deep, across, planes, lines = plan(n_ctx, n_tp)
+    in_plane, reach = deep * across, lines * deep
     rows = k_hbm.shape[0]
     width = k_hbm.shape[1]
     me = lax.axis_index("ctx") * n_tp + lax.axis_index("tp")
     core, chip = lax.rem(me, CORES), lax.div(me, CORES)
-    plane, spot = lax.div(chip, in_plane), lax.rem(chip, in_plane)
+    plane, x = lax.div(chip, in_plane), lax.rem(lax.div(chip, deep), across)
+    y = lax.rem(chip, deep)
 
     def device(other_chip, other_core):
         index = other_chip * CORES + other_core
@@ -42,8 +40,6 @@
 
     def piece(distance, from_core):
         return CORES * (reach - distance) + from_core
-
-    transit = CORES * (reach + 1)
 
     tall = rows // ROW_CUTS
 
@@ -64,13 +60,14 @@
     load_q.start()
 
     partner = device(chip, 1 - core)
-    around = [lax.rem(spot + o, in_plane) for o in range(1, in_plane)]
+    other_x = [lax.rem(x + o, across) for o in range(1, across)]
+    other_y = [lax.rem(y + o, deep) for o in range(1, deep)]
+    peers = [partner]
+    peers += [device(chip + (other - x) * deep, core) for other in other_x]
+    peers += [device(chip + other - y, core) for other in other_y]
     barrier = pltpu.get_barrier_semaphore()
-    pl.semaphore_signal(barrier, inc=1, device_id=partner, device_id_type=MESH)
-    for other in around:
-        pl.semaphore_signal(
-            barrier, inc=1, device_id=device(plane * in_plane + other, core), device_id_type=MESH
-        )
+    for peer in peers:
+        pl.semaphore_signal(barrier, inc=1, device_id=peer, device_id_type=MESH)
     below, above = plane > 0, plane < planes - 1
 
     @pl.when(below)
@@ -111,39 +108,48 @@
             kv[pl.ds(first, CORES * rows), :] = jnp.zeros((CORES * rows, 2 * width), kv.dtype)
 
     pl.semaphore_wait(
-        barrier, in_plane + below.astype(jnp.int32) + above.astype(jnp.int32)
+        barrier, len(peers) + below.astype(jnp.int32) + above.astype(jnp.int32)
     )
 
-    def forwards(level, source, held, chunk):
-        distance = level * in_plane
-        if level < levels:
-            following = distance + in_plane
-            index = piece(following, core) if following <= reach else transit + core
-            needed = following - spot <= reach
-            send(held & above & needed, chunk, source, device(chip + in_plane, core), index)
-        for other in around:
-            away = distance + other - spot
-            send(
-                held & (away >= 1) & (away <= reach),
-                chunk,
-                source,
-                device(plane * in_plane + other, core),
-                piece(jnp.clip(away, 1, reach), core),
-            )
-        if distance <= reach:
-            send(held, chunk, source, partner, piece(distance, core))
-
-    def pass_to_partner(when, distance):
-        index = piece(distance, core)
+    def hand_on(line, chunk):
+        index = piece(line * deep, core)
+        held = chip >= line * deep
+        if line + across <= lines:
+            straight = held if line == 0 else held & (line > x)
+            send(straight & above, chunk, index, device(chip + in_plane, core),
+                 piece((line + across) * deep, core))
+        if line in (0, across):
+            for other in other_x:
+                away = line + other - x
+                send(held & (away >= 1) & (away <= lines), chunk, index,
+                     device(chip + (other - x) * deep, core),
+                     piece(jnp.clip(away, 1, lines) * deep, core))
+        for other in other_y:
+            away = line * deep + other - y
+            send(held & (away >= 1) & (away <= reach), chunk, index,
+                 device(chip + other - y, core), piece(jnp.clip(away, 1, reach), core))
+        send(held, chunk, index, partner, index)
+
+    def line_in(line):
         for chunk in range(CHUNKS):
-            arrived(when, index, chunk)
-            send(when, chunk, index, partner, index)
+            arrived(chip >= line * deep, piece(line * deep, core), chunk)
+            hand_on(line, chunk)
+
+    def beside(line):
+        for off in range(1 - deep, deep):
+            back = line * deep + off
+            if off and 1 <= back <= reach:
+                when = (chip >= back) & (y - off >= 0) & (y - off < deep)
+                index = piece(back, core)
+                for chunk in range(CHUNKS):
+                    arrived(when, index, chunk)
+                    send(when, chunk, index, partner, index)
 
     load_k.wait()
     for chunk in range(CHUNKS):
         if chunk == ROW_CUTS:
             load_v.wait()
-        forwards(0, own, chip >= 0, chunk)
+        hand_on(0, chunk)
 
     keys = CORES * rows * (reach + 1)
     query_pos = me * rows + lax.broadcasted_iota(jnp.int32, (rows, keys), 0)
@@ -157,22 +163,16 @@
     bias[...] = jnp.where(visible, 0.0, -1e30)
     load_q.wait()
 
-    for level in range(1, levels + 1):
-        distance = level * in_plane
-        index = piece(distance, core) if distance <= reach else transit + core
-        held = (plane >= level) & (distance - spot <= reach)
-        if level > 1:
-            for back in range(1, min(reach, (level - 1) * in_plane - 1) + 1):
-                if back % in_plane:
-                    origin = lax.div(spot - back + 4 * in_plane, in_plane) - 4
-                    pass_to_partner((chip >= back) & (origin == 2 - level), back)
-        for chunk in range(CHUNKS):
-            arrived(held, index, chunk)
-            forwards(level, index, held, chunk)
-    for back in range(1, reach + 1):
-        if back % in_plane:
-            origin = lax.div(spot - back + 4 * in_plane, in_plane) - 4
-            pass_to_partner((chip >= back) & (origin <= 1 - levels), back)
+    line_in(across)
+    beside(0)
+    for line in range(1, across):
+        line_in(line)
+    beside(across)
+    for line in range(across + 1, lines + 1):
+        line_in(line)
+    for line in range(1, lines + 1):
+        if line != across:
+            beside(line)
     for distance in range(reach + 1):
         for chunk in range(CHUNKS):
             arrived(chip >= distance, piece(distance, 1 - core), chunk)
@@ -206,11 +206,11 @@
 
 
 def body(n_ctx, n_tp, queries, keys, values, doc_starts):
-    in_plane, planes, reach = plan(n_ctx, n_tp)
-    levels = (reach + in_plane - 1) // in_plane
+    deep, across, planes, lines = plan(n_ctx, n_tp)
+    reach = lines * deep
     rows, width = keys.shape
-    pieces = CORES * (reach + 2)
-    copies = (levels + 1) * (in_plane + 1) + levels * (reach + 1)
+    pieces = CORES * (reach + 1)
+    copies = (lines + 1) * (across + deep + 2 * deep)
     return pl.pallas_call(
         functools.partial(kernel, n_ctx, n_tp, doc_starts.shape[0]),
         out_shape=jax.ShapeDtypeStruct(queries.shape, queries.dtype),
@@ -225,7 +225,7 @@
             pltpu.SemaphoreType.DMA((copies * CHUNKS,)),
             pltpu.SemaphoreType.DMA((pieces, CHUNKS)),
         ],
-        compiler_params=pltpu.CompilerParams(collective_id=0, has_side_effects=True, vmem_limit_bytes=16 << 20),
+        compiler_params=pltpu.CompilerParams(collective_id=0, has_side_effects=True, vmem_limit_bytes=VMEM_BYTES),
     )(doc_starts, queries, keys, values)
 
 

time: 26.8 us -> 22.7 us (0.85)
  local copies, waits for them, and re-layouts: 4.17 us -> 1.87 us
  Pallas kernels: 22.4 us -> 20.6 us
    unnamed x9 -> x1, local copies, waits for them, and re-layouts: 4.17 us -> 1.87 us
    pallas_call x1, Pallas kernels: 22.4 us -> 20.6 us  [body(): pl.pallas_call(functools.partial(kernel, n_ctx, n_tp, doc_starts.shape[0]...]
where the time goes in v3:
time: 22.7 us; the launch traced here: 22.5 us
  Pallas kernels  20.6 us (91%)
  local copies, waits for them, and re-layouts  1.87 us (8%)
    pallas_call x1, Pallas kernels, body(): pl.pallas_call(functools.partial(kernel, n_ctx, n_tp, doc_starts.shape[0]...  20.6 us
    unnamed x1, local copies, waits for them, and re-layouts  1.87 us

profile of v3, /device:TPU:17, one launch (start us, length us, event | category | flops | bytes accessed | tf_op | source)
XLA Modules:
  0.0 22.5 jit_solution(9367758990176337248)
XLA Ops:
  0.0 20.6 %shard_map.46 = bf16[32,8192]{1,0:T(8,128)(2,1)} custom-call(s32[14]{0:T(128)} %docs.1, bf16[32,8192]{1,0:T(8,128)(2,1)} %q_hbm.1, bf16[32,1024]{1,0:T(8,128)(2,1)} %k_hbm.1, bf16[32,1024]{1,0:T(8,128)(2,1)} %v_hbm.1), custom_call_target="tpu_custom_call" | custom-call | tf_op jit(solution)/shard_map/pallas_call | solution.py:214
  20.6 1.9 %copy.6 = bf16[32,8192]{1,0:T(8,128)(2,1)} copy(bf16[32,8192]{1,0:T(8,128)(2,1)} %shard_map.46) | data formatting | bytes 1048576

commit v4 on v3

--- a/solution.py
+++ b/solution.py
@@ -126,7 +126,12 @@
                      piece(jnp.clip(away, 1, lines) * deep, core))
         for other in other_y:
             away = line * deep + other - y
-            send(held & (away >= 1) & (away <= reach), chunk, index,
+            wanted = held & (away >= 1) & (away <= reach)
+            if across > 1:
+                if line == 1:
+                    wanted &= x > 0
+                wanted &= (x < across - 1) | (away < in_plane) | (away >= in_plane + deep)
+            send(wanted, chunk, index,
                  device(chip + other - y, core), piece(jnp.clip(away, 1, reach), core))
         send(held, chunk, index, partner, index)
 
@@ -143,6 +148,13 @@
                 index = piece(back, core)
                 for chunk in range(CHUNKS):
                     arrived(when, index, chunk)
+                    last = when & (x == across - 1)
+                    if across > 1 and back < deep and back + in_plane <= reach:
+                        send(last & above, chunk, index, device(chip + in_plane, core),
+                             piece(back + in_plane, core))
+                    if across > 1 and line == across:
+                        send(last, chunk, index, device(chip - (across - 1) * deep, core),
+                             piece(deep + off, core))
                     send(when, chunk, index, partner, index)
 
     load_k.wait()
@@ -168,11 +180,12 @@
     for line in range(1, across):
         line_in(line)
     beside(across)
+    for line in range(1, across):
+        beside(line)
     for line in range(across + 1, lines + 1):
         line_in(line)
-    for line in range(1, lines + 1):
-        if line != across:
-            beside(line)
+    for line in range(across + 1, lines + 1):
+        beside(line)
     for distance in range(reach + 1):
         for chunk in range(CHUNKS):
             arrived(chip >= distance, piece(distance, 1 - core), chunk)
@@ -210,7 +223,7 @@
     reach = lines * deep
     rows, width = keys.shape
     pieces = CORES * (reach + 1)
-    copies = (lines + 1) * (across + deep + 2 * deep)
+    copies = (lines + 1) * 3 * deep + 2 * across + 4 * deep
     return pl.pallas_call(
         functools.partial(kernel, n_ctx, n_tp, doc_starts.shape[0]),
         out_shape=jax.ShapeDtypeStruct(queries.shape, queries.dtype),

time: 22.7 us -> 26.1 us (1.15)
  Pallas kernels: 20.6 us -> 24 us
    pallas_call x1, Pallas kernels: 20.6 us -> 24 us  [body(): pl.pallas_call(functools.partial(kernel, n_ctx, n_tp, doc_starts.shape[0]...]
where the time goes in v4:
time: 26.1 us; the launch traced here: 25.9 us
  Pallas kernels  24 us (92%)
  local copies, waits for them, and re-layouts  1.87 us (7%)
    pallas_call x1, Pallas kernels, body(): pl.pallas_call(functools.partial(kernel, n_ctx, n_tp, doc_starts.shape[0]...  24 us
    unnamed x1, local copies, waits for them, and re-layouts  1.87 us

profile of v4, /device:TPU:17, one launch (start us, length us, event | category | flops | bytes accessed | tf_op | source)
XLA Modules:
  0.0 25.9 jit_solution(3887750159300969247)
XLA Ops:
  0.0 24.0 %shard_map.46 = bf16[32,8192]{1,0:T(8,128)(2,1)} custom-call(s32[14]{0:T(128)} %docs.1, bf16[32,8192]{1,0:T(8,128)(2,1)} %q_hbm.1, bf16[32,1024]{1,0:T(8,128)(2,1)} %k_hbm.1, bf16[32,1024]{1,0:T(8,128)(2,1)} %v_hbm.1), custom_call_target="tpu_custom_call" | custom-call | tf_op jit(solution)/shard_map/pallas_call | solution.py:227
  24.1 1.9 %copy.6 = bf16[32,8192]{1,0:T(8,128)(2,1)} copy(bf16[32,8192]{1,0:T(8,128)(2,1)} %shard_map.46) | data formatting | bytes 1048576
